TPU v7x, 1024 devices: a whole 4x8x16 slice. The times are simulated.
1024 devices in a mesh: pp: 8 (over z_lo, core), tp: 16 (over z_hi, x), dp: 8 (over y).
Axes of the slice: x: 4, y: 8, z: 16 (z_hi: 4, z_lo: 4; z = z_hi * 4 + z_lo), core: 2. Of those that a mesh axis runs over, the one named last changes fastest.
Arguments:
- act_in: bfloat16 [8, 8, 128, 4096], P('pp', 'dp', 'tp'), may hold values from -6 to 6
- stash_in: bfloat16 [8, 8, 128, 4096], P('pp', 'dp', 'tp'), may hold values from -6 to 6
- grad_in: bfloat16 [8, 8, 128, 4096], P('pp', 'dp', 'tp'), may hold values from -6 to 6
- doc_ids: int32 [8, 8, 2, 128], P('pp', 'dp'), may hold values from 0 to 15, never falling along the last dimension, each value on 1 to 64 neighbouring positions
- query_weight: bfloat16 [8, 4096, 4096], P('pp', None, 'tp'), as said below
- key_weight: bfloat16 [8, 4096, 2048], P('pp', None, 'tp'), as said below
- value_weight: bfloat16 [8, 4096, 2048], P('pp', None, 'tp'), as said below
- out_weight: bfloat16 [8, 4096, 4096], P('pp', None, 'tp'), may hold values from -0.09375 to 0.09375
Outputs:
- act_out: bfloat16 [8, 8, 128, 4096], P('pp', 'dp', 'tp')
- grad_out: bfloat16 [8, 8, 128, 4096], P('pp', 'dp', 'tp')
- grad_query: float32 [8, 4096, 4096], P('pp', 'dp', 'tp')
- grad_key: float32 [8, 4096, 2048], P('pp', 'dp', 'tp')
- grad_value: float32 [8, 4096, 2048], P('pp', 'dp', 'tp')
Inputs may be any that keep to these rules, and one draw needn't show every extreme that they name: `doc_ids`: along each row of 128 positions the document numbers never fall. `query_weight`: entries of mean zero. `key_weight`: for each of the 8 key heads, its 2 stored copies (consecutive blocks of 128 columns) are equal; entries of mean zero. `value_weight`: for each of the 8 value heads, its 2 stored copies (consecutive blocks of 128 columns) are equal.
All inputs are finite; a program needn't handle non-finite values.
Results may differ from a plain program's by a relative error of at most 0.033.
Values may be sent and summed in bfloat16 or wider, within the bound.
No kernel may reach another device: no remote copies, remote signals or barrier semaphores. Data moves between devices by JAX's collectives and lax.ppermute only.
A program may use at most 64 MiB of HBM per device.

v0:
```python
import math

import jax
import jax.numpy as jnp
from jax import lax
from jax.experimental import pallas as pl
from jax.experimental.pallas import tpu as pltpu
from jax.sharding import Mesh, PartitionSpec as P


HEAD = 128
SCALE = 1.0 / math.sqrt(HEAD)
STRIPE = 512
epsilon = 1e-05
bf16 = jnp.bfloat16
f32 = jnp.float32


def shift(value, axis, steps):
    count = lax.axis_size(axis)
    return lax.ppermute(value, axis, [(i, (i + steps) % count) for i in range(count)])


def swap(blocks, axis):
    return lax.all_to_all(blocks, axis, 0, 0, tiled=True)


def dot(a, b, left, right):
    return lax.dot_general(a, b, (((left,), (right,)), ((), ())), preferred_element_type=f32)


def nn(a, b):
    return dot(a, b, 1, 0)


def nt(a, b):
    return dot(a, b, 1, 1)


def tn(a, b):
    return dot(a, b, 0, 0)


def kernel(fn, out, scratch, *args, flops=0, room=16):
    vmem = pl.BlockSpec(memory_space=pltpu.VMEM)
    smem = pl.BlockSpec(memory_space=pltpu.SMEM)
    size = sum(a.size * a.dtype.itemsize for a in args)
    return pl.pallas_call(
        fn,
        out_shape=out,
        in_specs=[smem if a.shape == (1,) else vmem for a in args],
        out_specs=jax.tree.map(lambda _: vmem, out),
        scratch_shapes=scratch,
        compiler_params=pltpu.CompilerParams(vmem_limit_bytes=room << 20),
        cost_estimate=pl.CostEstimate(flops=flops, bytes_accessed=size, transcendentals=0),
    )(*args)


def struct(shape, dtype=bf16):
    return jax.ShapeDtypeStruct(shape, dtype)


def unit(rows):
    wide = rows.astype(f32)
    inverse = lax.rsqrt(jnp.mean(wide * wide, axis=-1, keepdims=True) + epsilon)
    return wide * inverse, inverse


def norm_body(stash, grad, act, out):
    width = act.shape[1]
    out[:, :width] = unit(stash[...])[0].astype(bf16)
    out[:, width : 2 * width] = grad[...]
    out[:, 2 * width :] = unit(act[...])[0].astype(bf16)


def bias_of(here, docs, share):
    seq = docs.shape[1]
    count = 4
    wide = seq // count

    def position(axis):
        row = lax.broadcasted_iota(jnp.int32, (seq, seq), axis)
        step = row // wide
        at_x = lax.rem(here + step, count)
        at_z = (row - step * wide) // share
        return (at_z * count + at_x) * share + lax.rem(row, share)

    pick = (lax.broadcasted_iota(jnp.int32, (seq, seq), 1) == position(0)).astype(f32)
    lined = jnp.broadcast_to(docs.astype(f32), (8, seq))
    down = nt(pick, lined)[:, :1]
    along = nt(lined, pick)[:1, :]
    return jnp.where((position(1) <= position(0)) & (down == along), 0.0, -jnp.inf).astype(f32)


def softmax(queries, keys, bias):
    scores = nt(queries, keys) * SCALE + bias
    weights = jnp.exp(scores - jnp.max(scores, axis=-1, keepdims=True))
    return (weights / jnp.sum(weights, axis=-1, keepdims=True)).astype(bf16)


def lay(pieces, at, width, rows_ref):
    share = pieces[0].shape[0]
    for k, piece in enumerate(pieces):
        rows_ref[k * share : (k + 1) * share, :] = piece[:, at : at + width]


def forward_body(here, docs, p0, p1, p2, p3, w_q, w_k, w_v, w_o, o0, o1, o2, o3, rows):
    width = rows.shape[1]
    lay((p0, p1, p2, p3), 0, width, rows)
    bias = bias_of(here[0], docs[0:1, :], p0.shape[0] // 4)
    queries = nn(rows[...], w_q[...]).astype(bf16)
    keys = nn(rows[...], w_k[...]).astype(bf16)
    values = nn(rows[...], w_v[...]).astype(bf16)
    mixed = [
        nn(softmax(queries[:, h : h + HEAD], keys, bias), values).astype(bf16)
        for h in range(0, queries.shape[1], HEAD)
    ]
    mixed = jnp.concatenate(mixed, axis=1)
    for c in range(0, width, STRIPE):
        term = nt(mixed, w_o[c : c + STRIPE, :]).astype(bf16)
        share = o0.shape[0]
        for k, out in enumerate((o0, o1, o2, o3)):
            out[:, c : c + STRIPE] = term[k * share : (k + 1) * share]


def backward_body(
    here, docs, p0, p1, p2, p3, w_q, w_k, w_v, w_o, o0, o1, o2, o3, exchange, rows, grads
):
    width = rows.shape[1]
    lay((p0, p1, p2, p3), 0, width, rows)
    lay((p0, p1, p2, p3), width, width, grads)
    bias = bias_of(here[0], docs[1:2, :], p0.shape[0] // 4)
    queries = nn(rows[...], w_q[...]).astype(bf16)
    keys = nn(rows[...], w_k[...]).astype(bf16)
    values = nn(rows[...], w_v[...]).astype(bf16)
    dmixed = nn(grads[...], w_o[...]).astype(bf16)
    dqueries, dkeys, dvalues = [], 0.0, 0.0
    for h in range(0, queries.shape[1], HEAD):
        q, dm = queries[:, h : h + HEAD], dmixed[:, h : h + HEAD]
        probs = softmax(q, keys, bias)
        wide = probs.astype(f32)
        dprobs = nt(dm, values)
        inner = jnp.sum(wide * dprobs, axis=-1, keepdims=True)
        dscores = (wide * (dprobs - inner) * SCALE).astype(bf16)
        dqueries.append(nn(dscores, keys).astype(bf16))
        dkeys = dkeys + tn(dscores, q)
        dvalues = dvalues + tn(probs, dm)
    dqueries = jnp.concatenate(dqueries, axis=1)
    dkeys, dvalues = dkeys.astype(bf16), dvalues.astype(bf16)
    for c in range(0, width, STRIPE):
        at = slice(c, c + STRIPE)
        term = nt(dqueries, w_q[at, :]) + nt(dkeys, w_k[at, :]) + nt(dvalues, w_v[at, :])
        term = term.astype(bf16)
        share = o0.shape[0]
        for k, out in enumerate((o0, o1, o2, o3)):
            out[:, at] = term[k * share : (k + 1) * share]
    columns = jnp.concatenate([dqueries, dkeys, dvalues], axis=1)
    part = exchange.shape[2] - columns.shape[1]
    for c in range(exchange.shape[0]):
        exchange[c, :, :part] = rows[:, c * part : (c + 1) * part]
        exchange[c, :, part:] = columns


def half_body(here, a0, a1, a2, a3, o0, o1, o2, o3):
    count = a0.shape[0]
    for k, out in enumerate((o0, o1, o2, o3)):
        at = lax.rem(here[0] + k, count)
        total = a0[at].astype(f32) + a1[at].astype(f32) + a2[at].astype(f32) + a3[at].astype(f32)
        out[...] = total.astype(bf16)


def back_tail(a0, a1, a2, a3, stash, grad, out):
    dnormed = sum(ref[...].astype(f32) for ref in (a0, a1, a2, a3))
    scaled, inverse = unit(stash[...])
    slope = jnp.mean(dnormed * scaled, axis=-1, keepdims=True)
    out[...] = (grad[...].astype(f32) + inverse * (dnormed - scaled * slope)).astype(bf16)


def ahead_tail(a0, a1, a2, a3, act, out):
    attended = sum(ref[...].astype(f32) for ref in (a0, a1, a2, a3))
    out[...] = (act[...].astype(f32) + attended).astype(bf16)


def weights_body(exchange, g_q, g_k, g_v):
    part, nq, nk = g_q.shape[0], g_q.shape[1], g_k.shape[1]
    for out, at in ((g_q, 0), (g_k, nq), (g_v, nq + nk)):
        total = 0.0
        for c in range(exchange.shape[0]):
            columns = exchange[c, :, part + at : part + at + out.shape[1]]
            total = total + tn(exchange[c, :, :part], columns)
        out[...] = total


def collect(block, axis):
    count = lax.axis_size(axis)
    steps = sorted(range(1, count), key=lambda k: min(k, count - k))
    found = {step: shift(block, axis, -step) for step in steps}
    return [block] + [found[step] for step in range(1, count)]


def deal(blocks, axis):
    count = lax.axis_size(axis)
    steps = sorted(range(1, count), key=lambda k: min(k, count - k))
    return [blocks[0]] + [shift(blocks[step], axis, step) for step in steps]


def body(act_in, stash_in, grad_in, doc_ids, query_weight, key_weight, value_weight, out_weight):
    nz, nx, nd = lax.axis_size("tz"), lax.axis_size("tx"), lax.axis_size("dp")
    act, stash, grad = act_in[0, 0], stash_in[0, 0], grad_in[0, 0]
    matrices = (query_weight[0], key_weight[0], value_weight[0], out_weight[0])
    nq, nk = query_weight.shape[2], key_weight.shape[2]
    share, width = act.shape
    seq = share * nz * nx
    place = lax.axis_index("tz").astype(jnp.int32).reshape(1)
    here = lax.axis_index("tx").astype(jnp.int32).reshape(1)
    docs = doc_ids[0, 0]

    tall = pltpu.VMEM((seq, width), bf16)
    piece = struct((seq // nx, width))

    def halves(pieces):
        cut = [p.reshape(nz, share, width) for p in pieces]
        return kernel(half_body, [struct((share, width))] * nz, [], place, *cut, flops=1 << 22)

    mine = struct((share, 3 * width))
    mine = kernel(norm_body, mine, [], stash, grad, act, flops=1 << 22, room=8)
    by_z = lax.all_gather(mine, "tz", axis=0, tiled=True)
    behind, ahead = by_z[:, : 2 * width], by_z[:, 2 * width :]
    behind = collect(behind, "tx")
    ahead = collect(ahead, "tx")

    *partial, exchange = kernel(
        backward_body,
        [piece] * nx + [struct((nd, seq, width // nd + nq + 2 * nk))],
        [tall, tall],
        here, docs, *behind, *matrices,
        flops=2 * seq * width * (3 * nq + 4 * nk),
    )
    exchange = swap(exchange, "dp")
    partial = deal(partial, "tx")
    partial = halves(partial)
    partial = deal(partial, "tz")
    grad_back = kernel(back_tail, struct((share, width)), [], *partial, stash, grad, room=8)
    grad_out = shift(grad_back, "pp", -1)

    partial = kernel(
        forward_body,
        [piece] * nx,
        [tall],
        here, docs, *ahead, *matrices,
        flops=2 * seq * width * (2 * nq + 2 * nk),
    )
    partial = deal(partial, "tx")
    partial = halves(partial)
    partial = deal(partial, "tz")
    outgoing = kernel(ahead_tail, struct((share, width)), [], *partial, act, room=8)
    act_out = shift(outgoing, "pp", 1)

    part = width // nd
    grads = kernel(
        weights_body,
        [struct((part, n), f32) for n in (nq, nk, nk)],
        [],
        exchange,
        flops=2 * nd * seq * part * (nq + 2 * nk),
    )
    return (act_out[None, None], grad_out[None, None], *(g[None] for g in grads))


def solution(mesh):
    sizes = dict(mesh.shape)
    nz = 4
    grid = mesh.devices.reshape(sizes["pp"], nz, sizes["tp"] // nz, sizes["dp"])
    split = Mesh(grid, ("pp", "tz", "tx", "dp"))
    rows = P("pp", "dp", ("tz", "tx"), None)
    cols = P("pp", None, ("tz", "tx"))
    grads = P("pp", "dp", ("tz", "tx"))
    return jax.shard_map(
        body,
        mesh=split,
        in_specs=(rows, rows, rows, P("pp", "dp", None, None), cols, cols, cols, cols),
        out_specs=(rows, rows, grads, grads, grads),
        check_vma=False,
    )
```

profile of v0, /device:TPU:137, one launch (start us, length us, event | category | flops | bytes accessed | tf_op | source)
XLA Modules:
  0.0 203.6 jit_solution(8370502358366402157)
XLA Ops:
  3.5 44.1 %all_gather.3 = bf16[32,12288]{1,0:T(8,128)(2,1)} all-gather(bf16[8,12288]{1,0:T(8,128)(2,1)S(1)} %shard_map.119), channel_id=1, replica_groups=mesh['pp'=8,'tz'=4,'tx'=4,'dp'=8] {'tz'}, dimensions={0}, use_global_device_ids=true | all-gather | bytes 983040 | tf_op jit(solution)/shard_map/all_gather | solution.py:227
  48.6 4.4 %collective-permute-start.10 = (bf16[32,8192]{1,0:T(8,128)(2,1)S(1)}, bf16[32,8192]{1,0:T(8,128)(2,1)S(1)}, u32[]{:S(2)}, u32[]{:S(2)}) collective-permute-start(bf16[32,8192]{1,0:T(8,128)(2,1)S(1)} %slice.9.p0), channel_id=1, source_target_pairs={{0,24},{8,0},{16,8},{24,16},{1,25},{9,1},{17,9},{25,17},{2,26},{10... | collective-permute-start | bytes 1572872 | tf_op jit(solution)/shard_map/ppermute | solution.py:21
  53.0 2.4 %collective-permute-start.11 = (bf16[32,8192]{1,0:T(8,128)(2,1)S(1)}, bf16[32,8192]{1,0:T(8,128)(2,1)}, u32[]{:S(2)}, u32[]{:S(2)}) collective-permute-start(bf16[32,8192]{1,0:T(8,128)(2,1)S(1)} %slice.9.p0), channel_id=1, source_target_pairs={{0,16},{8,24},{16,0},{24,8},{1,17},{9,25},{17,1},{25,9},{2,18},{10... | collective-permute-start | bytes 1572872 | tf_op jit(solution)/shard_map/ppermute | solution.py:21
  55.4 2.5 %collective-permute-start.12 = (bf16[32,8192]{1,0:T(8,128)(2,1)S(1)}, bf16[32,8192]{1,0:T(8,128)(2,1)}, u32[]{:S(2)}, u32[]{:S(2)}) collective-permute-start(bf16[32,8192]{1,0:T(8,128)(2,1)S(1)} %slice.9.p0), channel_id=1, source_target_pairs={{0,8},{8,16},{16,24},{24,0},{1,9},{9,17},{17,25},{25,1},{2,10},{10... | collective-permute-start | bytes 1572872 | tf_op jit(solution)/shard_map/ppermute | solution.py:21
  58.0 6.4 %collective-permute-done.10.p1 = bf16[32,8192]{1,0:T(8,128)(2,1)S(1)} collective-permute-done((bf16[32,8192]{1,0:T(8,128)(2,1)S(1)}, bf16[32,8192]{1,0:T(8,128)(2,1)S(1)}, u32[]{:S(2)}, u32[]{:S(2)}) %collective-permute-start.10) | collective-permute-done | bytes 524320 | tf_op jit(solution)/shard_map/ppermute | solution.py:21
  64.3 4.7 %collective-permute-done.11.p2 = bf16[32,8192]{1,0:T(8,128)(2,1)} collective-permute-done((bf16[32,8192]{1,0:T(8,128)(2,1)S(1)}, bf16[32,8192]{1,0:T(8,128)(2,1)}, u32[]{:S(2)}, u32[]{:S(2)}) %collective-permute-start.11) | collective-permute-done | bytes 524320 | tf_op jit(solution)/shard_map/ppermute | solution.py:21
  69.0 12.6 %collective-permute-done.12.p3 = bf16[32,8192]{1,0:T(8,128)(2,1)} collective-permute-done((bf16[32,8192]{1,0:T(8,128)(2,1)S(1)}, bf16[32,8192]{1,0:T(8,128)(2,1)}, u32[]{:S(2)}, u32[]{:S(2)}) %collective-permute-start.12) | collective-permute-done | bytes 524320 | tf_op jit(solution)/shard_map/ppermute | solution.py:21
  81.6 1.6 copy-done.1
  85.6 5.9 %shard_map.123 = (bf16[32,4096]{1,0:T(8,128)(2,1)S(1)}, bf16[32,4096]{1,0:T(8,128)(2,1)}, bf16[32,4096]{1,0:T(8,128)(2,1)}, bf16[32,4096]{1,0:T(8,128)(2,1)}, bf16[8,128,1024]{2,1,0:T(8,128)(2,1)S(1)}) custom-call(s32[1]{0:T(128)} %bitcast.1.here, s32[2,128]{1,0:T(2,128)S(1)} %bitcast.45, bf16[32,8192]{1,0:T(8,128)(2,1)S(1)} %slice.9.p0, ...), custom_call_target="tpu_custom_call" | custom-call | flops 1342177280 | bytes 8389636 | tf_op jit(solution)/shard_map/pallas_call | solution.py:48
  92.9 7.1 %all-to-all-start = ((bf16[8,128,1024]{2,1,0:T(8,128)(2,1)}), bf16[8,128,1024]{2,1,0:T(8,128)(2,1)}, u32[]{:S(2)}, u32[]{:S(2)}) async-start(bf16[8,128,1024]{2,1,0:T(8,128)(2,1)} %copy-done.7), calls=%async_computation | async-start | bytes 4194304 | tf_op jit(solution)/shard_map/all_to_all | solution.py:25
  101.0 1.9 collective-permute-start
  102.9 2.4 %collective-permute-start.1 = (bf16[32,4096]{1,0:T(8,128)(2,1)S(1)}, bf16[32,4096]{1,0:T(8,128)(2,1)S(1)}, u32[]{:S(2)}, u32[]{:S(2)}) collective-permute-start(bf16[32,4096]{1,0:T(8,128)(2,1)S(1)} %slice.8.p0), channel_id=1, source_target_pairs={{0,16},{8,24},{16,0},{24,8},{1,17},{9,25},{17,1},{25,9},{2,18},{10... | collective-permute-start | bytes 786440 | tf_op jit(solution)/shard_map/ppermute | solution.py:21
  105.4 2.9 %collective-permute-start.2 = (bf16[32,4096]{1,0:T(8,128)(2,1)S(1)}, bf16[32,4096]{1,0:T(8,128)(2,1)S(1)}, u32[]{:S(2)}, u32[]{:S(2)}) collective-permute-start(bf16[32,4096]{1,0:T(8,128)(2,1)S(1)} %slice.8.p0), channel_id=1, source_target_pairs={{0,8},{8,16},{16,24},{24,0},{1,9},{9,17},{17,25},{25,1},{2,10},{10... | collective-permute-start | bytes 786440 | tf_op jit(solution)/shard_map/ppermute | solution.py:21
  109.8 2.8 %collective-permute-done.1.p2 = bf16[32,4096]{1,0:T(8,128)(2,1)S(1)} collective-permute-done((bf16[32,4096]{1,0:T(8,128)(2,1)S(1)}, bf16[32,4096]{1,0:T(8,128)(2,1)S(1)}, u32[]{:S(2)}, u32[]{:S(2)}) %collective-permute-start.1) | collective-permute-done | bytes 262176 | tf_op jit(solution)/shard_map/ppermute | solution.py:21
  112.6 7.4 %collective-permute-done.2.p3 = bf16[32,4096]{1,0:T(8,128)(2,1)S(1)} collective-permute-done((bf16[32,4096]{1,0:T(8,128)(2,1)S(1)}, bf16[32,4096]{1,0:T(8,128)(2,1)S(1)}, u32[]{:S(2)}, u32[]{:S(2)}) %collective-permute-start.2) | collective-permute-done | bytes 262176 | tf_op jit(solution)/shard_map/ppermute | solution.py:21
  122.9 2.9 %shard_map.120 = (bf16[32,4096]{1,0:T(8,128)(2,1)S(1)}, bf16[32,4096]{1,0:T(8,128)(2,1)S(1)}, bf16[32,4096]{1,0:T(8,128)(2,1)}, bf16[32,4096]{1,0:T(8,128)(2,1)}) custom-call(s32[1]{0:T(128)} %bitcast.1.here, s32[2,128]{1,0:T(2,128)S(1)} %bitcast.46, bf16[32,4096]{1,0:T(8,128)(2,1)S(1)} %slice.8.p0, bf16[32,4096]{1,0:T(8,128)(2,1)S(1)} %collective-permute-done.p1, ...), custom_call_target="tpu_custom_call" | custom-call | flops 805306368 | bytes 7341060 | tf_op jit(solution)/shard_map/pallas_call | solution.py:48
  126.5 2.0 %collective-permute-start.3 = (bf16[32,4096]{1,0:T(8,128)(2,1)S(1)}, bf16[32,4096]{1,0:T(8,128)(2,1)S(1)}, u32[]{:S(2)}, u32[]{:S(2)}) collective-permute-start(bf16[32,4096]{1,0:T(8,128)(2,1)S(1)} %get-tuple-element.26), channel_id=1, source_target_pairs={{0,8},{8,16},{16,24},{24,0},{1,9},{9,17},{17,25},{25,1},{2,10},{10... | collective-permute-start | bytes 786440 | tf_op jit(solution)/shard_map/ppermute | solution.py:21
  128.5 4.6 %collective-permute-start.4 = (bf16[32,4096]{1,0:T(8,128)(2,1)}, bf16[32,4096]{1,0:T(8,128)(2,1)S(1)}, u32[]{:S(2)}, u32[]{:S(2)}) collective-permute-start(bf16[32,4096]{1,0:T(8,128)(2,1)} %get-tuple-element.27), channel_id=1, source_target_pairs={{0,24},{8,0},{16,8},{24,16},{1,25},{9,1},{17,9},{25,17},{2,26},{10... | collective-permute-start | bytes 786440 | tf_op jit(solution)/shard_map/ppermute | solution.py:21
  133.1 1.9 collective-permute-start.5
  135.0 2.5 %collective-permute-start.13 = (bf16[32,4096]{1,0:T(8,128)(2,1)}, bf16[32,4096]{1,0:T(8,128)(2,1)S(1)}, u32[]{:S(2)}, u32[]{:S(2)}) collective-permute-start(bf16[32,4096]{1,0:T(8,128)(2,1)} %get-tuple-element.34), channel_id=1, source_target_pairs={{0,8},{8,16},{16,24},{24,0},{1,9},{9,17},{17,25},{25,1},{2,10},{10... | collective-permute-start | bytes 786440 | tf_op jit(solution)/shard_map/ppermute | solution.py:21
  137.5 4.0 %collective-permute-start.14 = (bf16[32,4096]{1,0:T(8,128)(2,1)}, bf16[32,4096]{1,0:T(8,128)(2,1)S(1)}, u32[]{:S(2)}, u32[]{:S(2)}) collective-permute-start(bf16[32,4096]{1,0:T(8,128)(2,1)} %get-tuple-element.35), channel_id=1, source_target_pairs={{0,24},{8,0},{16,8},{24,16},{1,25},{9,1},{17,9},{25,17},{2,26},{10... | collective-permute-start | bytes 786440 | tf_op jit(solution)/shard_map/ppermute | solution.py:21
  141.6 3.7 %collective-permute-start.15 = (bf16[32,4096]{1,0:T(8,128)(2,1)}, bf16[32,4096]{1,0:T(8,128)(2,1)S(1)}, u32[]{:S(2)}, u32[]{:S(2)}) collective-permute-start(bf16[32,4096]{1,0:T(8,128)(2,1)} %get-tuple-element.36), channel_id=1, source_target_pairs={{0,16},{8,24},{16,0},{24,8},{1,17},{9,25},{17,1},{25,9},{2,18},{10... | collective-permute-start | bytes 786440 | tf_op jit(solution)/shard_map/ppermute | solution.py:21
  146.3 5.8 %collective-permute-start.6 = (bf16[8,4096]{1,0:T(8,128)(2,1)S(1)}, bf16[8,4096]{1,0:T(8,128)(2,1)S(1)}, u32[]{:S(2)}, u32[]{:S(2)}) collective-permute-start(bf16[8,4096]{1,0:T(8,128)(2,1)S(1)} %get-tuple-element.30), channel_id=1, source_target_pairs={{0,32},{32,64},{64,96},{96,0},{1,33},{33,65},{65,97},{97,1},{2,34}... | collective-permute-start | bytes 196616 | tf_op jit(solution)/shard_map/ppermute | solution.py:21
  152.1 3.4 %collective-permute-start.7 = (bf16[8,4096]{1,0:T(8,128)(2,1)S(1)}, bf16[8,4096]{1,0:T(8,128)(2,1)S(1)}, u32[]{:S(2)}, u32[]{:S(2)}) collective-permute-start(bf16[8,4096]{1,0:T(8,128)(2,1)S(1)} %get-tuple-element.31), channel_id=1, source_target_pairs={{0,96},{32,0},{64,32},{96,64},{1,97},{33,1},{65,33},{97,65},{2,98}... | collective-permute-start | bytes 196616 | tf_op jit(solution)/shard_map/ppermute | solution.py:21
  155.6 7.5 %collective-permute-start.8 = (bf16[8,4096]{1,0:T(8,128)(2,1)S(1)}, bf16[8,4096]{1,0:T(8,128)(2,1)S(1)}, u32[]{:S(2)}, u32[]{:S(2)}) collective-permute-start(bf16[8,4096]{1,0:T(8,128)(2,1)S(1)} %get-tuple-element.32), channel_id=1, source_target_pairs={{0,64},{32,96},{64,0},{96,32},{1,65},{33,97},{65,1},{97,33},{2,66}... | collective-permute-start | bytes 196616 | tf_op jit(solution)/shard_map/ppermute | solution.py:21
  163.3 5.8 %collective-permute-start.16 = (bf16[8,4096]{1,0:T(8,128)(2,1)S(1)}, bf16[8,4096]{1,0:T(8,128)(2,1)S(1)}, u32[]{:S(2)}, u32[]{:S(2)}) collective-permute-start(bf16[8,4096]{1,0:T(8,128)(2,1)S(1)} %get-tuple-element.38), channel_id=1, source_target_pairs={{0,32},{32,64},{64,96},{96,0},{1,33},{33,65},{65,97},{97,1},{2,34}... | collective-permute-start | bytes 196616 | tf_op jit(solution)/shard_map/ppermute | solution.py:21
  169.0 3.4 %collective-permute-start.17 = (bf16[8,4096]{1,0:T(8,128)(2,1)S(1)}, bf16[8,4096]{1,0:T(8,128)(2,1)S(1)}, u32[]{:S(2)}, u32[]{:S(2)}) collective-permute-start(bf16[8,4096]{1,0:T(8,128)(2,1)S(1)} %get-tuple-element.39), channel_id=1, source_target_pairs={{0,96},{32,0},{64,32},{96,64},{1,97},{33,1},{65,33},{97,65},{2,98}... | collective-permute-start | bytes 196616 | tf_op jit(solution)/shard_map/ppermute | solution.py:21
  172.5 6.5 %collective-permute-start.18 = (bf16[8,4096]{1,0:T(8,128)(2,1)S(1)}, bf16[8,4096]{1,0:T(8,128)(2,1)S(1)}, u32[]{:S(2)}, u32[]{:S(2)}) collective-permute-start(bf16[8,4096]{1,0:T(8,128)(2,1)S(1)} %get-tuple-element.40), channel_id=1, source_target_pairs={{0,64},{32,96},{64,0},{96,32},{1,65},{33,97},{65,1},{97,33},{2,66}... | collective-permute-start | bytes 196616 | tf_op jit(solution)/shard_map/ppermute | solution.py:21
  179.0 8.4 %collective-permute-start.9 = (bf16[8,4096]{1,0:T(8,128)(2,1)S(1)}, bf16[8,4096]{1,0:T(8,128)(2,1)S(1)}, u32[]{:S(2)}, u32[]{:S(2)}) collective-permute-start(bf16[8,4096]{1,0:T(8,128)(2,1)S(1)} %shard_map.122), channel_id=1, source_target_pairs={{0,128},{128,256},{256,384},{384,512},{512,640},{640,768},{768,896... | collective-permute-start | bytes 196616 | tf_op jit(solution)/shard_map/ppermute | solution.py:21
  187.8 5.5 %collective-permute-start.19 = (bf16[8,4096]{1,0:T(8,128)(2,1)S(1)}, bf16[8,4096]{1,0:T(8,128)(2,1)S(1)}, u32[]{:S(2)}, u32[]{:S(2)}) collective-permute-start(bf16[8,4096]{1,0:T(8,128)(2,1)S(1)} %shard_map.125), channel_id=1, source_target_pairs={{0,896},{128,0},{256,128},{384,256},{512,384},{640,512},{768,640},... | collective-permute-start | bytes 196616 | tf_op jit(solution)/shard_map/ppermute | solution.py:21
  193.3 5.3 %collective-permute-done.19 = bf16[8,4096]{1,0:T(8,128)(2,1)S(1)} collective-permute-done((bf16[8,4096]{1,0:T(8,128)(2,1)S(1)}, bf16[8,4096]{1,0:T(8,128)(2,1)S(1)}, u32[]{:S(2)}, u32[]{:S(2)}) %collective-permute-start.19) | collective-permute-done | bytes 65568 | tf_op jit(solution)/shard_map/ppermute | solution.py:21
  198.5 3.7 %shard_map.126 = (f32[512,256]{1,0:T(8,128)}, f32[512,128]{1,0:T(8,128)}, f32[512,128]{1,0:T(8,128)}) custom-call(bf16[8,128,1024]{2,1,0:T(8,128)(2,1)} %all-to-all-done.exchange), custom_call_target="tpu_custom_call" | custom-call | flops 536870912 | bytes 2097152 | tf_op jit(solution)/shard_map/pallas_call | solution.py:48
  (57 shorter events, 16.6 us)
Async XLA Ops:
  0.6 81.0 %copy-start = (bf16[1,4096,256]{2,1,0:T(8,128)(2,1)S(1)}, bf16[1,4096,256]{2,1,0:T(8,128)(2,1)}, u32[]{:S(2)}) copy-start(bf16[1,4096,256]{2,1,0:T(8,128)(2,1)} %param.12) | copy-start | bytes 6291460
  3.3 78.3 %copy-start.16 = (s32[1,1,2,128]{3,2,1,0:T(2,128)S(1)}, s32[1,1,2,128]{3,2,1,0:T(2,128)}, u32[]{:S(2)}) copy-start(s32[1,1,2,128]{3,2,1,0:T(2,128)} %param.11) | copy-start | bytes 3076
  48.6 15.7 %collective-permute-start.10 = (bf16[32,8192]{1,0:T(8,128)(2,1)S(1)}, bf16[32,8192]{1,0:T(8,128)(2,1)S(1)}, u32[]{:S(2)}, u32[]{:S(2)}) collective-permute-start(bf16[32,8192]{1,0:T(8,128)(2,1)S(1)} %slice.9.p0), channel_id=1, source_target_pairs={{0,24},{8,0},{16,8},{24,16},{1,25},{9,1},{17,9},{25,17},{2,26},{10... | collective-permute-start | bytes 1572872 | tf_op jit(solution)/shard_map/ppermute | solution.py:21
  53.0 16.0 %collective-permute-start.11 = (bf16[32,8192]{1,0:T(8,128)(2,1)S(1)}, bf16[32,8192]{1,0:T(8,128)(2,1)}, u32[]{:S(2)}, u32[]{:S(2)}) collective-permute-start(bf16[32,8192]{1,0:T(8,128)(2,1)S(1)} %slice.9.p0), channel_id=1, source_target_pairs={{0,16},{8,24},{16,0},{24,8},{1,17},{9,25},{17,1},{25,9},{2,18},{10... | collective-permute-start | bytes 1572872 | tf_op jit(solution)/shard_map/ppermute | solution.py:21
  55.4 26.1 %collective-permute-start.12 = (bf16[32,8192]{1,0:T(8,128)(2,1)S(1)}, bf16[32,8192]{1,0:T(8,128)(2,1)}, u32[]{:S(2)}, u32[]{:S(2)}) collective-permute-start(bf16[32,8192]{1,0:T(8,128)(2,1)S(1)} %slice.9.p0), channel_id=1, source_target_pairs={{0,8},{8,16},{16,24},{24,0},{1,9},{9,17},{17,25},{25,1},{2,10},{10... | collective-permute-start | bytes 1572872 | tf_op jit(solution)/shard_map/ppermute | solution.py:21
  81.6 1.6 copy-start.1
  83.2 1.2 copy-start.3
  84.4 1.2 copy-start.5
  91.6 1.3 copy-start.7
  92.9 27.2 %copy-start.4 = (bf16[1,4096,128]{2,1,0:T(8,128)(2,1)S(1)}, bf16[1,4096,128]{2,1,0:T(8,128)(2,1)}, u32[]{:S(2)}) copy-start(bf16[1,4096,128]{2,1,0:T(8,128)(2,1)} %param.13) | copy-start | bytes 3145732
  92.9 105.6 %all-to-all-start = ((bf16[8,128,1024]{2,1,0:T(8,128)(2,1)}), bf16[8,128,1024]{2,1,0:T(8,128)(2,1)}, u32[]{:S(2)}, u32[]{:S(2)}) async-start(bf16[8,128,1024]{2,1,0:T(8,128)(2,1)} %copy-done.7), calls=%async_computation | async-start | bytes 4194304 | tf_op jit(solution)/shard_map/all_to_all | solution.py:25
  101.0 8.8 %collective-permute-start = (bf16[32,4096]{1,0:T(8,128)(2,1)S(1)}, bf16[32,4096]{1,0:T(8,128)(2,1)S(1)}, u32[]{:S(2)}, u32[]{:S(2)}) collective-permute-start(bf16[32,4096]{1,0:T(8,128)(2,1)S(1)} %slice.8.p0), channel_id=1, source_target_pairs={{0,24},{8,0},{16,8},{24,16},{1,25},{9,1},{17,9},{25,17},{2,26},{10... | collective-permute-start | bytes 786440 | tf_op jit(solution)/shard_map/ppermute | solution.py:21
  102.9 9.7 %collective-permute-start.1 = (bf16[32,4096]{1,0:T(8,128)(2,1)S(1)}, bf16[32,4096]{1,0:T(8,128)(2,1)S(1)}, u32[]{:S(2)}, u32[]{:S(2)}) collective-permute-start(bf16[32,4096]{1,0:T(8,128)(2,1)S(1)} %slice.8.p0), channel_id=1, source_target_pairs={{0,16},{8,24},{16,0},{24,8},{1,17},{9,25},{17,1},{25,9},{2,18},{10... | collective-permute-start | bytes 786440 | tf_op jit(solution)/shard_map/ppermute | solution.py:21
  105.4 14.7 %collective-permute-start.2 = (bf16[32,4096]{1,0:T(8,128)(2,1)S(1)}, bf16[32,4096]{1,0:T(8,128)(2,1)S(1)}, u32[]{:S(2)}, u32[]{:S(2)}) collective-permute-start(bf16[32,4096]{1,0:T(8,128)(2,1)S(1)} %slice.8.p0), channel_id=1, source_target_pairs={{0,8},{8,16},{16,24},{24,0},{1,9},{9,17},{17,25},{25,1},{2,10},{10... | collective-permute-start | bytes 786440 | tf_op jit(solution)/shard_map/ppermute | solution.py:21
  120.1 1.6 copy-start.2
  122.9 56.1 %copy-start.15 = (bf16[1,1,8,4096]{3,2,1,0:T(8,128)(2,1)S(1)}, bf16[1,1,8,4096]{3,2,1,0:T(8,128)(2,1)}, u32[]{:S(2)}) copy-start(bf16[1,1,8,4096]{3,2,1,0:T(8,128)(2,1)} %param.8) | copy-start | bytes 196612
  126.5 61.0 %copy-start.9 = (bf16[1,1,8,4096]{3,2,1,0:T(8,128)(2,1)S(1)}, bf16[1,1,8,4096]{3,2,1,0:T(8,128)(2,1)}, u32[]{:S(2)}) copy-start(bf16[1,1,8,4096]{3,2,1,0:T(8,128)(2,1)} %param.9) | copy-start | bytes 196612
  126.5 61.0 %copy-start.11 = (bf16[1,1,8,4096]{3,2,1,0:T(8,128)(2,1)S(1)}, bf16[1,1,8,4096]{3,2,1,0:T(8,128)(2,1)}, u32[]{:S(2)}) copy-start(bf16[1,1,8,4096]{3,2,1,0:T(8,128)(2,1)} %param.10) | copy-start | bytes 196612
  126.5 15.1 %collective-permute-start.3 = (bf16[32,4096]{1,0:T(8,128)(2,1)S(1)}, bf16[32,4096]{1,0:T(8,128)(2,1)S(1)}, u32[]{:S(2)}, u32[]{:S(2)}) collective-permute-start(bf16[32,4096]{1,0:T(8,128)(2,1)S(1)} %get-tuple-element.26), channel_id=1, source_target_pairs={{0,8},{8,16},{16,24},{24,0},{1,9},{9,17},{17,25},{25,1},{2,10},{10... | collective-permute-start | bytes 786440 | tf_op jit(solution)/shard_map/ppermute | solution.py:21
  128.5 16.7 %collective-permute-start.4 = (bf16[32,4096]{1,0:T(8,128)(2,1)}, bf16[32,4096]{1,0:T(8,128)(2,1)S(1)}, u32[]{:S(2)}, u32[]{:S(2)}) collective-permute-start(bf16[32,4096]{1,0:T(8,128)(2,1)} %get-tuple-element.27), channel_id=1, source_target_pairs={{0,24},{8,0},{16,8},{24,16},{1,25},{9,1},{17,9},{25,17},{2,26},{10... | collective-permute-start | bytes 786440 | tf_op jit(solution)/shard_map/ppermute | solution.py:21
  133.1 12.1 %collective-permute-start.5 = (bf16[32,4096]{1,0:T(8,128)(2,1)}, bf16[32,4096]{1,0:T(8,128)(2,1)S(1)}, u32[]{:S(2)}, u32[]{:S(2)}) collective-permute-start(bf16[32,4096]{1,0:T(8,128)(2,1)} %get-tuple-element.28), channel_id=1, source_target_pairs={{0,16},{8,24},{16,0},{24,8},{1,17},{9,25},{17,1},{25,9},{2,18},{10... | collective-permute-start | bytes 786440 | tf_op jit(solution)/shard_map/ppermute | solution.py:21
  135.0 20.5 %collective-permute-start.13 = (bf16[32,4096]{1,0:T(8,128)(2,1)}, bf16[32,4096]{1,0:T(8,128)(2,1)S(1)}, u32[]{:S(2)}, u32[]{:S(2)}) collective-permute-start(bf16[32,4096]{1,0:T(8,128)(2,1)} %get-tuple-element.34), channel_id=1, source_target_pairs={{0,8},{8,16},{16,24},{24,0},{1,9},{9,17},{17,25},{25,1},{2,10},{10... | collective-permute-start | bytes 786440 | tf_op jit(solution)/shard_map/ppermute | solution.py:21
  137.5 25.6 %collective-permute-start.14 = (bf16[32,4096]{1,0:T(8,128)(2,1)}, bf16[32,4096]{1,0:T(8,128)(2,1)S(1)}, u32[]{:S(2)}, u32[]{:S(2)}) collective-permute-start(bf16[32,4096]{1,0:T(8,128)(2,1)} %get-tuple-element.35), channel_id=1, source_target_pairs={{0,24},{8,0},{16,8},{24,16},{1,25},{9,1},{17,9},{25,17},{2,26},{10... | collective-permute-start | bytes 786440 | tf_op jit(solution)/shard_map/ppermute | solution.py:21
  141.6 21.5 %collective-permute-start.15 = (bf16[32,4096]{1,0:T(8,128)(2,1)}, bf16[32,4096]{1,0:T(8,128)(2,1)S(1)}, u32[]{:S(2)}, u32[]{:S(2)}) collective-permute-start(bf16[32,4096]{1,0:T(8,128)(2,1)} %get-tuple-element.36), channel_id=1, source_target_pairs={{0,16},{8,24},{16,0},{24,8},{1,17},{9,25},{17,1},{25,9},{2,18},{10... | collective-permute-start | bytes 786440 | tf_op jit(solution)/shard_map/ppermute | solution.py:21
  146.3 26.1 %collective-permute-start.6 = (bf16[8,4096]{1,0:T(8,128)(2,1)S(1)}, bf16[8,4096]{1,0:T(8,128)(2,1)S(1)}, u32[]{:S(2)}, u32[]{:S(2)}) collective-permute-start(bf16[8,4096]{1,0:T(8,128)(2,1)S(1)} %get-tuple-element.30), channel_id=1, source_target_pairs={{0,32},{32,64},{64,96},{96,0},{1,33},{33,65},{65,97},{97,1},{2,34}... | collective-permute-start | bytes 196616 | tf_op jit(solution)/shard_map/ppermute | solution.py:21
  152.1 26.8 %collective-permute-start.7 = (bf16[8,4096]{1,0:T(8,128)(2,1)S(1)}, bf16[8,4096]{1,0:T(8,128)(2,1)S(1)}, u32[]{:S(2)}, u32[]{:S(2)}) collective-permute-start(bf16[8,4096]{1,0:T(8,128)(2,1)S(1)} %get-tuple-element.31), channel_id=1, source_target_pairs={{0,96},{32,0},{64,32},{96,64},{1,97},{33,1},{65,33},{97,65},{2,98}... | collective-permute-start | bytes 196616 | tf_op jit(solution)/shard_map/ppermute | solution.py:21
  155.6 23.4 %collective-permute-start.8 = (bf16[8,4096]{1,0:T(8,128)(2,1)S(1)}, bf16[8,4096]{1,0:T(8,128)(2,1)S(1)}, u32[]{:S(2)}, u32[]{:S(2)}) collective-permute-start(bf16[8,4096]{1,0:T(8,128)(2,1)S(1)} %get-tuple-element.32), channel_id=1, source_target_pairs={{0,64},{32,96},{64,0},{96,32},{1,65},{33,97},{65,1},{97,33},{2,66}... | collective-permute-start | bytes 196616 | tf_op jit(solution)/shard_map/ppermute | solution.py:21
  163.3 24.2 %collective-permute-start.16 = (bf16[8,4096]{1,0:T(8,128)(2,1)S(1)}, bf16[8,4096]{1,0:T(8,128)(2,1)S(1)}, u32[]{:S(2)}, u32[]{:S(2)}) collective-permute-start(bf16[8,4096]{1,0:T(8,128)(2,1)S(1)} %get-tuple-element.38), channel_id=1, source_target_pairs={{0,32},{32,64},{64,96},{96,0},{1,33},{33,65},{65,97},{97,1},{2,34}... | collective-permute-start | bytes 196616 | tf_op jit(solution)/shard_map/ppermute | solution.py:21
  169.0 18.4 %collective-permute-start.17 = (bf16[8,4096]{1,0:T(8,128)(2,1)S(1)}, bf16[8,4096]{1,0:T(8,128)(2,1)S(1)}, u32[]{:S(2)}, u32[]{:S(2)}) collective-permute-start(bf16[8,4096]{1,0:T(8,128)(2,1)S(1)} %get-tuple-element.39), channel_id=1, source_target_pairs={{0,96},{32,0},{64,32},{96,64},{1,97},{33,1},{65,33},{97,65},{2,98}... | collective-permute-start | bytes 196616 | tf_op jit(solution)/shard_map/ppermute | solution.py:21
  172.5 15.0 %collective-permute-start.18 = (bf16[8,4096]{1,0:T(8,128)(2,1)S(1)}, bf16[8,4096]{1,0:T(8,128)(2,1)S(1)}, u32[]{:S(2)}, u32[]{:S(2)}) collective-permute-start(bf16[8,4096]{1,0:T(8,128)(2,1)S(1)} %get-tuple-element.40), channel_id=1, source_target_pairs={{0,64},{32,96},{64,0},{96,32},{1,65},{33,97},{65,1},{97,33},{2,66}... | collective-permute-start | bytes 196616 | tf_op jit(solution)/shard_map/ppermute | solution.py:21
  179.0 14.2 %collective-permute-start.9 = (bf16[8,4096]{1,0:T(8,128)(2,1)S(1)}, bf16[8,4096]{1,0:T(8,128)(2,1)S(1)}, u32[]{:S(2)}, u32[]{:S(2)}) collective-permute-start(bf16[8,4096]{1,0:T(8,128)(2,1)S(1)} %shard_map.122), channel_id=1, source_target_pairs={{0,128},{128,256},{256,384},{384,512},{512,640},{640,768},{768,896... | collective-permute-start | bytes 196616 | tf_op jit(solution)/shard_map/ppermute | solution.py:21
  187.8 10.8 %collective-permute-start.19 = (bf16[8,4096]{1,0:T(8,128)(2,1)S(1)}, bf16[8,4096]{1,0:T(8,128)(2,1)S(1)}, u32[]{:S(2)}, u32[]{:S(2)}) collective-permute-start(bf16[8,4096]{1,0:T(8,128)(2,1)S(1)} %shard_map.125), channel_id=1, source_target_pairs={{0,896},{128,0},{256,128},{384,256},{512,384},{640,512},{768,640},... | collective-permute-start | bytes 196616 | tf_op jit(solution)/shard_map/ppermute | solution.py:21
  (6 other events, 5.5 us)
where the time goes:
time: 205 us; the launch traced here: 204 us
  starting transfers between devices  88.6 us (43%)
  blocking collectives  44.1 us (22%)
  waiting for transfers between devices  40.8 us (20%)
  local copies, waits for them, and re-layouts  15.8 us (8%)
  Pallas kernels  13.3 us (6%)
    ppermute x20, starting transfers between devices, shift(): lax.ppermute(value, axis, [(i, (i + steps) % count) for i in range(count)])  81.5 us
    all_gather x1, blocking collectives, body(): by_z = lax.all_gather(mine, 'tz', axis=0, tiled=True)  44.1 us
    ppermute x20, waiting for transfers between devices, shift(): lax.ppermute(value, axis, [(i, (i + steps) % count) for i in range(count)])  40.8 us
    unnamed x36, local copies, waits for them, and re-layouts  13.8 us
    pallas_call x8, Pallas kernels, kernel(): pl.pallas_call(fn, out_shape=out, in_specs=[smem if a.shape == (1,) else...  13.3 us
    all_to_all x1, starting transfers between devices, swap(): return lax.all_to_all(blocks, axis, 0, 0, tiled=True)  7.12 us
  transfers between devices with their start and end apart: 21, of which 7 were waited for; matrix products, arithmetic and copies ran while one was open for 0% of the time, Pallas kernels for 2%

commit v1 on v0

v1 whole, which is shorter than its diff:
```python
import math

import jax
import jax.numpy as jnp
from jax import lax
from jax.experimental import pallas as pl
from jax.experimental.pallas import tpu as pltpu
from jax.sharding import Mesh, PartitionSpec as P


HEAD = 128
SCALE = 1.0 / math.sqrt(HEAD)
STRIPE = 512
epsilon = 1e-05
bf16 = jnp.bfloat16
f32 = jnp.float32


def shift(value, axis, steps):
    count = lax.axis_size(axis)
    return lax.ppermute(value, axis, [(i, (i + steps) % count) for i in range(count)])


def dot(a, b, left, right):
    return lax.dot_general(a, b, (((left,), (right,)), ((), ())), preferred_element_type=f32)


def nn(a, b):
    return dot(a, b, 1, 0)


def nt(a, b):
    return dot(a, b, 1, 1)


def tn(a, b):
    return dot(a, b, 0, 0)


def kernel(fn, out, scratch, *args, flops=0, room=16, space=pltpu.VMEM):
    taken, vmem = pl.BlockSpec(memory_space=space), pl.BlockSpec(memory_space=pltpu.VMEM)
    smem = pl.BlockSpec(memory_space=pltpu.SMEM)
    size = sum(a.size * a.dtype.itemsize for a in args)
    return pl.pallas_call(
        fn,
        out_shape=out,
        in_specs=[smem if a.shape == (1,) else taken for a in args],
        out_specs=jax.tree.map(lambda _: vmem, out),
        scratch_shapes=scratch,
        compiler_params=pltpu.CompilerParams(vmem_limit_bytes=room << 20),
        cost_estimate=pl.CostEstimate(flops=flops, bytes_accessed=size, transcendentals=0),
    )(*args)


def struct(shape, dtype=bf16):
    return jax.ShapeDtypeStruct(shape, dtype)


def unit(rows):
    wide = rows.astype(f32)
    inverse = lax.rsqrt(jnp.mean(wide * wide, axis=-1, keepdims=True) + epsilon)
    return wide * inverse, inverse


def norm_body(stash, grad, act, out, held, sems):
    width = act.shape[1]
    copies = [
        pltpu.make_async_copy(ref, held.at[k], sems.at[k])
        for k, ref in enumerate((stash, act))
    ]
    copies.append(pltpu.make_async_copy(grad, held.at[2], sems.at[2]))
    for copy in copies:
        copy.start()
    for k, at in enumerate((0, 2)):
        copies[k].wait()
        out[:, at * width : (at + 1) * width] = unit(held[k])[0].astype(bf16)
    copies[2].wait()
    out[:, width : 2 * width] = held[2]


def bias_of(here, docs, share):
    seq = docs.shape[1]
    count = 4
    wide = seq // count

    def position(axis):
        row = lax.broadcasted_iota(jnp.int32, (seq, seq), axis)
        step = row // wide
        at_x = lax.rem(here + step, count)
        at_z = (row - step * wide) // share
        return (at_z * count + at_x) * share + lax.rem(row, share)

    pick = (lax.broadcasted_iota(jnp.int32, (seq, seq), 1) == position(0)).astype(f32)
    lined = jnp.broadcast_to(docs.astype(f32), (8, seq))
    down = nt(pick, lined)[:, :1]
    along = nt(lined, pick)[:1, :]
    return jnp.where((position(1) <= position(0)) & (down == along), 0.0, -jnp.inf).astype(f32)


def softmax(queries, keys, bias):
    scores = nt(queries, keys) * SCALE + bias
    weights = jnp.exp(scores - jnp.max(scores, axis=-1, keepdims=True))
    return (weights / jnp.sum(weights, axis=-1, keepdims=True)).astype(bf16)


def fetch_body(*refs):
    count = (len(refs) - 1) // 2
    copies = []
    for k in range(count):
        rows = refs[k].shape[0] // 4
        for part in range(4):
            at = pl.ds(part * rows, rows)
            copies.append(
                pltpu.make_async_copy(
                    refs[k].at[at], refs[count + k].at[at], refs[-1].at[4 * k + part]
                )
            )
    for copy in copies:
        copy.start()
    for copy in copies:
        copy.wait()


def lay(pieces, at, width, rows_ref):
    share = pieces[0].shape[0]
    for k, piece in enumerate(pieces):
        rows_ref[k * share : (k + 1) * share, :] = piece[:, at : at + width]


def run_forward(bias, queries, keys, values, w_o, outs):
    width = w_o.shape[0]
    mixed = [
        nn(softmax(queries[:, h : h + HEAD], keys, bias), values).astype(bf16)
        for h in range(0, queries.shape[1], HEAD)
    ]
    mixed = jnp.concatenate(mixed, axis=1)
    for c in range(0, width, STRIPE):
        term = nt(mixed, w_o[c : c + STRIPE, :]).astype(bf16)
        share = outs[0].shape[0]
        for k, out in enumerate(outs):
            out[:, width + c : width + c + STRIPE] = term[k * share : (k + 1) * share]


def run_backward(bias, queries, keys, values, dmixed, w_q, w_k, w_v, outs):
    width = w_q.shape[0]
    dqueries, dkeys, dvalues = [], 0.0, 0.0
    for h in range(0, queries.shape[1], HEAD):
        q, dm = queries[:, h : h + HEAD], dmixed[:, h : h + HEAD]
        probs = softmax(q, keys, bias)
        wide = probs.astype(f32)
        dprobs = nt(dm, values)
        inner = jnp.sum(wide * dprobs, axis=-1, keepdims=True)
        dscores = (wide * (dprobs - inner) * SCALE).astype(bf16)
        dqueries.append(nn(dscores, keys).astype(bf16))
        dkeys = dkeys + tn(dscores, q)
        dvalues = dvalues + tn(probs, dm)
    dqueries = jnp.concatenate(dqueries, axis=1)
    dkeys, dvalues = dkeys.astype(bf16), dvalues.astype(bf16)
    for c in range(0, width, STRIPE):
        at = slice(c, c + STRIPE)
        term = nt(dqueries, w_q[at, :]) + nt(dkeys, w_k[at, :]) + nt(dvalues, w_v[at, :])
        term = term.astype(bf16)
        share = outs[0].shape[0]
        for k, out in enumerate(outs):
            out[:, at] = term[k * share : (k + 1) * share]
    return jnp.concatenate([dqueries, dkeys, dvalues], axis=1)


def both_body(here, docs, *refs):
    pieces, (w_q, w_k, w_v, w_o), outs = refs[:4], refs[4:8], refs[8:12]
    behind, columns, ahead, grads = refs[12:]
    width, share = grads.shape[1], pieces[0].shape[0] // 4
    lay(pieces, 0, width, behind)
    lay(pieces, width, width, grads)
    queries, keys, values = (nn(behind[...], w[...]).astype(bf16) for w in (w_q, w_k, w_v))
    dmixed = nn(grads[...], w_o[...]).astype(bf16)
    bias = bias_of(here[0], docs[1:2, :], share)
    columns[...] = run_backward(bias, queries, keys, values, dmixed, w_q, w_k, w_v, outs)
    lay(pieces, 2 * width, width, ahead)
    queries, keys, values = (nn(ahead[...], w[...]).astype(bf16) for w in (w_q, w_k, w_v))
    run_forward(bias_of(here[0], docs[0:1, :], share), queries, keys, values, w_o, outs)


def parcel_body(copy, behind, columns, *sent):
    part = behind.shape[1] // len(sent)
    for k, out in enumerate(sent):
        at = lax.rem(copy[0] + k, len(sent)) * part
        out[:, :part] = behind[:, pl.ds(pl.multiple_of(at, part), part)]
        out[:, part:] = columns[...]


def half_body(place, a0, a1, a2, a3, keep_b, send_b, keep_f, send_f):
    width = keep_b.shape[2]
    own, last = place[0], a0.shape[0] - 1
    beside = own + 1 - 2 * lax.rem(own, 2)
    plan = (
        (keep_b, 0, (own, last - own)),
        (send_b, 0, (beside, last - beside)),
        (keep_f, width, (own, beside)),
        (send_f, width, (last - own, last - beside)),
    )
    for out, at, chunks in plan:
        for k, chunk in enumerate(chunks):
            total = sum(a[chunk, :, at : at + width].astype(f32) for a in (a0, a1, a2, a3))
            out[k] = total.astype(bf16)


def through_norm(dnormed, scaled, inverse):
    return inverse * (dnormed - scaled * jnp.mean(dnormed * scaled, axis=-1, keepdims=True))


def join_back(keep, came, stash, beside, grad, own, other):
    first = through_norm(keep[0].astype(f32) + came[0].astype(f32), *unit(stash[...]))
    own[...] = (grad[...].astype(f32) + first).astype(bf16)
    second = through_norm(keep[1].astype(f32) + came[1].astype(f32), *unit(beside[...]))
    other[...] = second.astype(bf16)


def join_ahead(keep, came, act, own, other):
    own[...] = (act[...].astype(f32) + keep[0].astype(f32) + came[0].astype(f32)).astype(bf16)
    other[...] = (keep[1].astype(f32) + came[1].astype(f32)).astype(bf16)


def end_body(own, other, out):
    out[...] = (own[...].astype(f32) + other[...].astype(f32)).astype(bf16)


def weights_body(*refs):
    sent, (g_q, g_k, g_v) = refs[:-3], refs[-3:]
    part, nq, nk = g_q.shape[0], g_q.shape[1], g_k.shape[1]
    for out, at in ((g_q, 0), (g_k, nq), (g_v, nq + nk)):
        total = 0.0
        for one in sent:
            total = total + tn(one[:, :part], one[:, part + at : part + at + out.shape[1]])
        out[...] = total


def across(value, axis, mask):
    count = lax.axis_size(axis)
    return lax.ppermute(value, axis, [(i, i ^ mask) for i in range(count)])


def collect(block, axis):
    count = lax.axis_size(axis)
    steps = sorted(range(1, count), key=lambda k: min(k, count - k))
    found = {step: shift(block, axis, -step) for step in steps}
    return [block] + [found[step] for step in range(1, count)]


def slant(value, steps, mask):
    np, nz = lax.axis_size("pp"), lax.axis_size("tz")
    pairs = [
        (p * nz + z, (p + steps) % np * nz + (z ^ mask)) for p in range(np) for z in range(nz)
    ]
    return lax.ppermute(value, ("pp", "tz"), pairs)


def deal(blocks, axis):
    count = lax.axis_size(axis)
    steps = sorted(range(1, count), key=lambda k: min(k, count - k))
    return [blocks[0]] + [shift(blocks[step], axis, step) for step in steps]


def body(act_in, stash_in, grad_in, doc_ids, query_weight, key_weight, value_weight, out_weight):
    nz, nx, nd = lax.axis_size("tz"), lax.axis_size("tx"), lax.axis_size("dp")
    act, stash, grad = act_in[0, 0], stash_in[0, 0], grad_in[0, 0]
    matrices = (query_weight[0], key_weight[0], value_weight[0], out_weight[0])
    nq, nk = query_weight.shape[2], key_weight.shape[2]
    share, width = act.shape
    seq, part = share * nz * nx, width // nd
    here, place, copy = (
        lax.axis_index(axis).astype(jnp.int32).reshape(1) for axis in ("tx", "tz", "dp")
    )

    mine = kernel(
        norm_body,
        struct((share, 3 * width)),
        [pltpu.VMEM((3, share, width), bf16), pltpu.SemaphoreType.DMA((3,))],
        stash, grad, act,
        flops=1 << 22, room=8, space=pltpu.HBM,
    )
    by_z = lax.all_gather(mine, "tz", axis=0, tiled=True)
    pieces = collect(by_z, "tx")
    beside = across(stash, "tz", nz - 1)
    matrices = kernel(
        fetch_body,
        [struct(m.shape) for m in matrices],
        [pltpu.SemaphoreType.DMA((16,))],
        *matrices,
        flops=1 << 22, room=4, space=pltpu.HBM,
    )
    tall = pltpu.VMEM((seq, width), bf16)
    outs = [struct((seq // nx, 2 * width))] * nx
    *partial, behind, columns = kernel(
        both_body,
        outs + [struct((seq, width)), struct((seq, nq + 2 * nk))],
        [tall, tall],
        here, doc_ids[0, 0], *pieces, *matrices,
        flops=2 * seq * width * (5 * nq + 6 * nk), room=24,
    )
    partial = deal(partial, "tx")
    parcels = kernel(
        parcel_body, [struct((seq, part + nq + 2 * nk))] * nd, [],
        copy, behind, columns, flops=1 << 22, room=4,
    )
    far = sorted(range(1, nd), key=lambda k: -min(k, nd - k))
    sent = [parcels[0]]
    for steps in (far[:4], far[4:]):
        sent += [shift(parcels[step], "dp", step) for step in steps]
    pair = struct((2, share, width))
    partial = [p.reshape(nz, share, 2 * width) for p in partial]
    keep_b, send_b, keep_f, send_f = kernel(
        half_body, [pair] * 4, [], place, *partial, flops=1 << 23, room=8
    )
    came_b = across(send_b, "tz", 1)
    came_f = across(send_f, "tz", nz - 1)
    row = struct((share, width))
    own_b, other_b = kernel(
        join_back, [row, row], [], keep_b, came_b, stash, beside, grad, flops=1 << 20, room=4
    )
    other_b, own_b = slant(other_b, -1, nz - 1), shift(own_b, "pp", -1)
    own_f, other_f = kernel(join_ahead, [row, row], [], keep_f, came_f, act, flops=1 << 20, room=4)
    other_f, own_f = slant(other_f, 1, 1), shift(own_f, "pp", 1)
    grad_out = kernel(end_body, row, [], own_b, other_b, flops=1 << 20, room=4)[None, None]
    act_out = kernel(end_body, row, [], own_f, other_f, flops=1 << 20, room=4)[None, None]
    grads = kernel(
        weights_body,
        [struct((part, n), f32) for n in (nq, nk, nk)],
        [],
        *sent,
        flops=2 * nd * seq * part * (nq + 2 * nk),
    )
    return (act_out, grad_out, *(g[None] for g in grads))


def solution(mesh):
    sizes = dict(mesh.shape)
    nz = 4
    grid = mesh.devices.reshape(sizes["pp"], nz, sizes["tp"] // nz, sizes["dp"])
    split = Mesh(grid, ("pp", "tz", "tx", "dp"))
    rows = P("pp", "dp", ("tz", "tx"), None)
    cols = P("pp", None, ("tz", "tx"))
    grads = P("pp", "dp", ("tz", "tx"))
    return jax.shard_map(
        body,
        mesh=split,
        in_specs=(rows, rows, rows, P("pp", "dp", None, None), cols, cols, cols, cols),
        out_specs=(rows, rows, grads, grads, grads),
        check_vma=False,
    )
```

time: 205 us -> 210 us (1.024)
  the two profiles are of different devices: /device:TPU:137 before, /device:TPU:46 now
where the time goes in v1:
time: 210 us; the launch traced here: 209 us
  starting transfers between devices  78.1 us (37%)
  waiting for transfers between devices  61.6 us (29%)
  blocking collectives  42.2 us (20%)
  Pallas kernels  14.1 us (7%)
  local copies, waits for them, and re-layouts  11.7 us (6%)
    ppermute x15, starting transfers between devices, shift(): lax.ppermute(value, axis, [(i, (i + steps) % count) for i in range(count)])  56.5 us
    ppermute x15, waiting for transfers between devices, shift(): lax.ppermute(value, axis, [(i, (i + steps) % count) for i in range(count)])  44 us
    all_gather x1, blocking collectives, body(): by_z = lax.all_gather(mine, 'tz', axis=0, tiled=True)  42.2 us
    pallas_call x10, Pallas kernels, kernel(): pl.pallas_call(fn, out_shape=out, in_specs=[smem if a.shape == (1,) else...  14.1 us
    ppermute x3, waiting for transfers between devices, across(): return lax.ppermute(value, axis, [(i, i ^ mask) for i in range(count)])  12.6 us
    ppermute x3, starting transfers between devices, across(): return lax.ppermute(value, axis, [(i, i ^ mask) for i in range(count)])  12.1 us
    unnamed x42, local copies, waits for them, and re-layouts  11.7 us
    ppermute x2, starting transfers between devices, slant(): return lax.ppermute(value, ('pp', 'tz'), pairs)  9.51 us
  transfers between devices with their start and end apart: 20, of which 7 were waited for; matrix products, arithmetic and copies ran while one was open for 0% of the time, Pallas kernels for 2%

profile of v1, /device:TPU:46, one launch (start us, length us, event | category | flops | bytes accessed | tf_op | source)
XLA Modules:
  0.0 208.7 jit_solution(2409334076173429995)
XLA Ops:
  3.8 42.2 %all_gather.3.refs_0_ = bf16[32,12288]{1,0:T(8,128)(2,1)S(1)} all-gather(bf16[8,12288]{1,0:T(8,128)(2,1)S(1)} %shard_map.119), channel_id=1, replica_groups=mesh['pp'=8,'tz'=4,'tx'=4,'dp'=8] {'tz'}, dimensions={0}, use_global_device_ids=true | all-gather | bytes 983040 | tf_op jit(solution)/shard_map/all_gather | solution.py:282
  46.0 2.7 %collective-permute-start = (bf16[32,12288]{1,0:T(8,128)(2,1)S(1)}, bf16[32,12288]{1,0:T(8,128)(2,1)S(1)}, u32[]{:S(2)}, u32[]{:S(2)}) collective-permute-start(bf16[32,12288]{1,0:T(8,128)(2,1)S(1)} %all_gather.3.refs_0_), channel_id=1, source_target_pairs={{0,24},{8,0},{16,8},{24,16},{1,25},{9,1},{17,9},{25,17},{2,26},{10... | collective-permute-start | bytes 2359304 | tf_op jit(solution)/shard_map/ppermute | solution.py:21
  48.7 3.0 %collective-permute-start.1 = (bf16[32,12288]{1,0:T(8,128)(2,1)S(1)}, bf16[32,12288]{1,0:T(8,128)(2,1)S(1)}, u32[]{:S(2)}, u32[]{:S(2)}) collective-permute-start(bf16[32,12288]{1,0:T(8,128)(2,1)S(1)} %all_gather.3.refs_0_), channel_id=1, source_target_pairs={{0,16},{8,24},{16,0},{24,8},{1,17},{9,25},{17,1},{25,9},{2,18},{10... | collective-permute-start | bytes 2359304 | tf_op jit(solution)/shard_map/ppermute | solution.py:21
  51.7 4.0 %collective-permute-start.2 = (bf16[32,12288]{1,0:T(8,128)(2,1)S(1)}, bf16[32,12288]{1,0:T(8,128)(2,1)}, u32[]{:S(2)}, u32[]{:S(2)}) collective-permute-start(bf16[32,12288]{1,0:T(8,128)(2,1)S(1)} %all_gather.3.refs_0_), channel_id=1, source_target_pairs={{0,8},{8,16},{16,24},{24,0},{1,9},{9,17},{17,25},{25,1},{2,10},{10... | collective-permute-start | bytes 2359304 | tf_op jit(solution)/shard_map/ppermute | solution.py:21
  55.8 1.6 copy-done
  57.4 1.6 copy-done.1
  60.8 19.6 %collective-permute-done.refs_1_ = bf16[32,12288]{1,0:T(8,128)(2,1)S(1)} collective-permute-done((bf16[32,12288]{1,0:T(8,128)(2,1)S(1)}, bf16[32,12288]{1,0:T(8,128)(2,1)S(1)}, u32[]{:S(2)}, u32[]{:S(2)}) %collective-permute-start) | collective-permute-done | bytes 786464 | tf_op jit(solution)/shard_map/ppermute | solution.py:21
  80.4 2.6 %collective-permute-done.2.refs_3_ = bf16[32,12288]{1,0:T(8,128)(2,1)} collective-permute-done((bf16[32,12288]{1,0:T(8,128)(2,1)S(1)}, bf16[32,12288]{1,0:T(8,128)(2,1)}, u32[]{:S(2)}, u32[]{:S(2)}) %collective-permute-start.2) | collective-permute-done | bytes 786464 | tf_op jit(solution)/shard_map/ppermute | solution.py:21
  83.0 8.0 %shard_map.121 = (bf16[32,8192]{1,0:T(8,128)(2,1)S(1)}, bf16[32,8192]{1,0:T(8,128)(2,1)}, bf16[32,8192]{1,0:T(8,128)(2,1)}, bf16[32,8192]{1,0:T(8,128)(2,1)}, bf...) custom-call(s32[1]{0:T(128)} %bitcast.1.here, s32[2,128]{1,0:T(2,128)S(1)} %bitcast.35, ...), custom_call_target="tpu_custom_call" | custom-call | flops 2147483648 | bytes 9438212 | tf_op jit(solution)/shard_map/pallas_call | solution.py:44
  91.8 4.6 %collective-permute-start.3 = (bf16[32,8192]{1,0:T(8,128)(2,1)}, bf16[32,8192]{1,0:T(8,128)(2,1)S(1)}, u32[]{:S(2)}, u32[]{:S(2)}) collective-permute-start(bf16[32,8192]{1,0:T(8,128)(2,1)} %get-tuple-element.39), channel_id=1, source_target_pairs={{0,8},{8,16},{16,24},{24,0},{1,9},{9,17},{17,25},{25,1},{2,10},{10... | collective-permute-start | bytes 1572872 | tf_op jit(solution)/shard_map/ppermute | solution.py:21
  96.5 1.9 collective-permute-start.4
  98.4 3.4 %collective-permute-start.5 = (bf16[32,8192]{1,0:T(8,128)(2,1)}, bf16[32,8192]{1,0:T(8,128)(2,1)S(1)}, u32[]{:S(2)}, u32[]{:S(2)}) collective-permute-start(bf16[32,8192]{1,0:T(8,128)(2,1)} %get-tuple-element.41), channel_id=1, source_target_pairs={{0,16},{8,24},{16,0},{24,8},{1,17},{9,25},{17,1},{25,9},{2,18},{10... | collective-permute-start | bytes 1572872 | tf_op jit(solution)/shard_map/ppermute | solution.py:21
  105.6 2.9 %collective-permute-start.13 = (bf16[128,1024]{1,0:T(8,128)(2,1)}, bf16[128,1024]{1,0:T(8,128)(2,1)S(1)}, u32[]{:S(2)}, u32[]{:S(2)}) collective-permute-start(bf16[128,1024]{1,0:T(8,128)(2,1)} %get-tuple-element.53), channel_id=1, source_target_pairs={{0,4},{1,5},{2,6},{3,7},{4,0},{5,1},{6,2},{7,3},{8,12},{9,13},{10,... | collective-permute-start | bytes 786440 | tf_op jit(solution)/shard_map/ppermute | solution.py:21
  108.5 6.7 %collective-permute-start.14 = (bf16[128,1024]{1,0:T(8,128)(2,1)}, bf16[128,1024]{1,0:T(8,128)(2,1)S(1)}, u32[]{:S(2)}, u32[]{:S(2)}) collective-permute-start(bf16[128,1024]{1,0:T(8,128)(2,1)} %get-tuple-element.54), channel_id=1, source_target_pairs={{0,3},{1,4},{2,5},{3,6},{4,7},{5,0},{6,1},{7,2},{8,11},{9,12},{10,... | collective-permute-start | bytes 786440 | tf_op jit(solution)/shard_map/ppermute | solution.py:21
  115.2 4.1 %collective-permute-done.3 = bf16[32,8192]{1,0:T(8,128)(2,1)S(1)} collective-permute-done((bf16[32,8192]{1,0:T(8,128)(2,1)}, bf16[32,8192]{1,0:T(8,128)(2,1)S(1)}, u32[]{:S(2)}, u32[]{:S(2)}) %collective-permute-start.3) | collective-permute-done | bytes 524320 | tf_op jit(solution)/shard_map/ppermute | solution.py:21
  119.4 5.2 %collective-permute-done.4 = bf16[32,8192]{1,0:T(8,128)(2,1)S(1)} collective-permute-done((bf16[32,8192]{1,0:T(8,128)(2,1)}, bf16[32,8192]{1,0:T(8,128)(2,1)S(1)}, u32[]{:S(2)}, u32[]{:S(2)}) %collective-permute-start.4) | collective-permute-done | bytes 524320 | tf_op jit(solution)/shard_map/ppermute | solution.py:21
  125.9 2.3 %collective-permute-start.9 = (bf16[2,8,4096]{2,1,0:T(8,128)(2,1)S(1)}, bf16[2,8,4096]{2,1,0:T(8,128)(2,1)S(1)}, u32[]{:S(2)}, u32[]{:S(2)}) collective-permute-start(bf16[2,8,4096]{2,1,0:T(8,128)(2,1)S(1)} %get-tuple-element.47), channel_id=1, source_target_pairs={{0,32},{32,0},{64,96},{96,64},{1,33},{33,1},{65,97},{97,65},{2,34}... | collective-permute-start | bytes 393224 | tf_op jit(solution)/shard_map/ppermute | solution.py:240
  128.3 7.2 %collective-permute-start.6 = (bf16[2,8,4096]{2,1,0:T(8,128)(2,1)S(1)}, bf16[2,8,4096]{2,1,0:T(8,128)(2,1)S(1)}, u32[]{:S(2)}, u32[]{:S(2)}) collective-permute-start(bf16[2,8,4096]{2,1,0:T(8,128)(2,1)S(1)} %get-tuple-element.43), channel_id=1, source_target_pairs={{0,96},{32,64},{64,32},{96,0},{1,97},{33,65},{65,33},{97,1},{2,98}... | collective-permute-start | bytes 393224 | tf_op jit(solution)/shard_map/ppermute | solution.py:240
  135.5 2.6 %collective-permute-start.10 = (bf16[8,4096]{1,0:T(8,128)(2,1)S(1)}, bf16[8,4096]{1,0:T(8,128)(2,1)S(1)}, u32[]{:S(2)}, u32[]{:S(2)}) collective-permute-start(bf16[8,4096]{1,0:T(8,128)(2,1)S(1)} %bitcast.31), channel_id=1, source_target_pairs={{0,96},{32,64},{64,32},{96,0},{1,97},{33,65},{65,33},{97,1},{2,98}... | collective-permute-start | bytes 196616 | tf_op jit(solution)/shard_map/ppermute | solution.py:240
  138.0 12.6 %collective-permute-done.10.beside = bf16[8,4096]{1,0:T(8,128)(2,1)S(1)} collective-permute-done((bf16[8,4096]{1,0:T(8,128)(2,1)S(1)}, bf16[8,4096]{1,0:T(8,128)(2,1)S(1)}, u32[]{:S(2)}, u32[]{:S(2)}) %collective-permute-start.10) | collective-permute-done | bytes 65568 | tf_op jit(solution)/shard_map/ppermute | solution.py:240
  150.6 3.0 %collective-permute-start.15 = (bf16[128,1024]{1,0:T(8,128)(2,1)S(1)}, bf16[128,1024]{1,0:T(8,128)(2,1)S(1)}, u32[]{:S(2)}, u32[]{:S(2)}) collective-permute-start(bf16[128,1024]{1,0:T(8,128)(2,1)S(1)} %copy-done.20), channel_id=1, source_target_pairs={{0,5},{1,6},{2,7},{3,0},{4,1},{5,2},{6,3},{7,4},{8,13},{9,14},{10,... | collective-permute-start | bytes 786440 | tf_op jit(solution)/shard_map/ppermute | solution.py:21
  153.7 4.5 %collective-permute-start.16 = (bf16[128,1024]{1,0:T(8,128)(2,1)S(1)}, bf16[128,1024]{1,0:T(8,128)(2,1)S(1)}, u32[]{:S(2)}, u32[]{:S(2)}) collective-permute-start(bf16[128,1024]{1,0:T(8,128)(2,1)S(1)} %copy-done.18), channel_id=1, source_target_pairs={{0,2},{1,3},{2,4},{3,5},{4,6},{5,7},{6,0},{7,1},{8,10},{9,11},{10,... | collective-permute-start | bytes 786440 | tf_op jit(solution)/shard_map/ppermute | solution.py:21
  158.2 3.5 %collective-permute-start.17 = (bf16[128,1024]{1,0:T(8,128)(2,1)S(1)}, bf16[128,1024]{1,0:T(8,128)(2,1)S(1)}, u32[]{:S(2)}, u32[]{:S(2)}) collective-permute-start(bf16[128,1024]{1,0:T(8,128)(2,1)S(1)} %copy-done.16), channel_id=1, source_target_pairs={{0,6},{1,7},{2,0},{3,1},{4,2},{5,3},{6,4},{7,5},{8,14},{9,15},{10,... | collective-permute-start | bytes 786440 | tf_op jit(solution)/shard_map/ppermute | solution.py:21
  161.7 2.3 %collective-permute-start.18 = (bf16[128,1024]{1,0:T(8,128)(2,1)S(1)}, bf16[128,1024]{1,0:T(8,128)(2,1)S(1)}, u32[]{:S(2)}, u32[]{:S(2)}) collective-permute-start(bf16[128,1024]{1,0:T(8,128)(2,1)S(1)} %copy-done.14), channel_id=1, source_target_pairs={{0,1},{1,2},{2,3},{3,4},{4,5},{5,6},{6,7},{7,0},{8,9},{9,10},{10,1... | collective-permute-start | bytes 786440 | tf_op jit(solution)/shard_map/ppermute | solution.py:21
  164.0 3.6 %collective-permute-start.19 = (bf16[128,1024]{1,0:T(8,128)(2,1)S(1)}, bf16[128,1024]{1,0:T(8,128)(2,1)S(1)}, u32[]{:S(2)}, u32[]{:S(2)}) collective-permute-start(bf16[128,1024]{1,0:T(8,128)(2,1)S(1)} %get-tuple-element.59), channel_id=1, source_target_pairs={{0,7},{1,0},{2,1},{3,2},{4,3},{5,4},{6,5},{7,6},{8,15},{9,8},{10,9... | collective-permute-start | bytes 786440 | tf_op jit(solution)/shard_map/ppermute | solution.py:21
  167.9 12.3 %collective-permute-done.15.refs_3_ = bf16[128,1024]{1,0:T(8,128)(2,1)S(1)} collective-permute-done((bf16[128,1024]{1,0:T(8,128)(2,1)S(1)}, bf16[128,1024]{1,0:T(8,128)(2,1)S(1)}, u32[]{:S(2)}, u32[]{:S(2)}) %collective-permute-start.15) | collective-permute-done | bytes 262176 | tf_op jit(solution)/shard_map/ppermute | solution.py:21
  180.2 8.2 %collective-permute-start.11 = (bf16[8,4096]{1,0:T(8,128)(2,1)S(1)}, bf16[8,4096]{1,0:T(8,128)(2,1)S(1)}, u32[]{:S(2)}, u32[]{:S(2)}) collective-permute-start(bf16[8,4096]{1,0:T(8,128)(2,1)S(1)} %get-tuple-element.48), channel_id=1, source_target_pairs={{0,896},{128,0},{256,128},{384,256},{512,384},{640,512},{768,640},... | collective-permute-start | bytes 196616 | tf_op jit(solution)/shard_map/ppermute | solution.py:21
  188.4 2.2 %collective-permute-start.12 = (bf16[8,4096]{1,0:T(8,128)(2,1)S(1)}, bf16[8,4096]{1,0:T(8,128)(2,1)S(1)}, u32[]{:S(2)}, u32[]{:S(2)}) collective-permute-start(bf16[8,4096]{1,0:T(8,128)(2,1)S(1)} %get-tuple-element.49), channel_id=1, source_target_pairs={{0,992},{32,960},{64,928},{96,896},{128,96},{160,64},{192,32},{224... | collective-permute-start | bytes 196616 | tf_op jit(solution)/shard_map/ppermute | solution.py:255
  190.6 2.2 %collective-permute-start.7 = (bf16[8,4096]{1,0:T(8,128)(2,1)S(1)}, bf16[8,4096]{1,0:T(8,128)(2,1)S(1)}, u32[]{:S(2)}, u32[]{:S(2)}) collective-permute-start(bf16[8,4096]{1,0:T(8,128)(2,1)S(1)} %get-tuple-element.44), channel_id=1, source_target_pairs={{0,128},{128,256},{256,384},{384,512},{512,640},{640,768},{768,896... | collective-permute-start | bytes 196616 | tf_op jit(solution)/shard_map/ppermute | solution.py:21
  192.8 7.3 %collective-permute-start.8 = (bf16[8,4096]{1,0:T(8,128)(2,1)S(1)}, bf16[8,4096]{1,0:T(8,128)(2,1)S(1)}, u32[]{:S(2)}, u32[]{:S(2)}) collective-permute-start(bf16[8,4096]{1,0:T(8,128)(2,1)S(1)} %get-tuple-element.45), channel_id=1, source_target_pairs={{0,160},{32,128},{64,224},{96,192},{128,288},{160,256},{192,352},{... | collective-permute-start | bytes 196616 | tf_op jit(solution)/shard_map/ppermute | solution.py:255
  200.2 2.2 %shard_map.128 = (f32[512,256]{1,0:T(8,128)}, f32[512,128]{1,0:T(8,128)}, f32[512,128]{1,0:T(8,128)}) custom-call(bf16[128,1024]{1,0:T(8,128)(2,1)S(1)} %get-tuple-element.52.refs_0_, bf16[128,1024]{1,0:T(8,128)(2,1)S(1)} %collective-permute-done.13.refs_1_, bf16[128,1024]{1,0:T(8,128)(2,1)S(1)} %collective-permute-done.14.refs_2_, ...), custom_call_target="tpu_custom_call" | custom-call | flops 536870912 | bytes 2097152 | tf_op jit(solution)/shard_map/pallas_call | solution.py:44
  203.0 5.1 %collective-permute-done.8.other = bf16[8,4096]{1,0:T(8,128)(2,1)S(1)} collective-permute-done((bf16[8,4096]{1,0:T(8,128)(2,1)S(1)}, bf16[8,4096]{1,0:T(8,128)(2,1)S(1)}, u32[]{:S(2)}, u32[]{:S(2)}) %collective-permute-start.8) | collective-permute-done | bytes 65568 | tf_op jit(solution)/shard_map/ppermute | solution.py:255
  (61 shorter events, 12.5 us)
Async XLA Ops:
  0.6 55.1 %copy-start.2 = (bf16[1,4096,128]{2,1,0:T(8,128)(2,1)S(1)}, bf16[1,4096,128]{2,1,0:T(8,128)(2,1)}, u32[]{:S(2)}) copy-start(bf16[1,4096,128]{2,1,0:T(8,128)(2,1)} %param.13) | copy-start | bytes 3145732
  46.0 34.4 %collective-permute-start = (bf16[32,12288]{1,0:T(8,128)(2,1)S(1)}, bf16[32,12288]{1,0:T(8,128)(2,1)S(1)}, u32[]{:S(2)}, u32[]{:S(2)}) collective-permute-start(bf16[32,12288]{1,0:T(8,128)(2,1)S(1)} %all_gather.3.refs_0_), channel_id=1, source_target_pairs={{0,24},{8,0},{16,8},{24,16},{1,25},{9,1},{17,9},{25,17},{2,26},{10... | collective-permute-start | bytes 2359304 | tf_op jit(solution)/shard_map/ppermute | solution.py:21
  48.7 31.7 %collective-permute-start.1 = (bf16[32,12288]{1,0:T(8,128)(2,1)S(1)}, bf16[32,12288]{1,0:T(8,128)(2,1)S(1)}, u32[]{:S(2)}, u32[]{:S(2)}) collective-permute-start(bf16[32,12288]{1,0:T(8,128)(2,1)S(1)} %all_gather.3.refs_0_), channel_id=1, source_target_pairs={{0,16},{8,24},{16,0},{24,8},{1,17},{9,25},{17,1},{25,9},{2,18},{10... | collective-permute-start | bytes 2359304 | tf_op jit(solution)/shard_map/ppermute | solution.py:21
  51.7 31.3 %collective-permute-start.2 = (bf16[32,12288]{1,0:T(8,128)(2,1)S(1)}, bf16[32,12288]{1,0:T(8,128)(2,1)}, u32[]{:S(2)}, u32[]{:S(2)}) collective-permute-start(bf16[32,12288]{1,0:T(8,128)(2,1)S(1)} %all_gather.3.refs_0_), channel_id=1, source_target_pairs={{0,8},{8,16},{16,24},{24,0},{1,9},{9,17},{17,25},{25,1},{2,10},{10... | collective-permute-start | bytes 2359304 | tf_op jit(solution)/shard_map/ppermute | solution.py:21
  55.8 1.6 copy-start
  57.3 1.6 copy-start.1
  58.9 1.2 copy-start.3
  60.2 22.9 %copy-start.12 = (s32[1,1,2,128]{3,2,1,0:T(2,128)S(1)}, s32[1,1,2,128]{3,2,1,0:T(2,128)}, u32[]{:S(2)}) copy-start(s32[1,1,2,128]{3,2,1,0:T(2,128)} %param.11) | copy-start | bytes 3076
  91.8 43.7 %copy-start.9 = (bf16[1,1,8,4096]{3,2,1,0:T(8,128)(2,1)S(1)}, bf16[1,1,8,4096]{3,2,1,0:T(8,128)(2,1)}, u32[]{:S(2)}) copy-start(bf16[1,1,8,4096]{3,2,1,0:T(8,128)(2,1)} %param.9) | copy-start | bytes 196612
  91.8 75.7 %copy-start.7 = (bf16[1,1,8,4096]{3,2,1,0:T(8,128)(2,1)S(1)}, bf16[1,1,8,4096]{3,2,1,0:T(8,128)(2,1)}, u32[]{:S(2)}) copy-start(bf16[1,1,8,4096]{3,2,1,0:T(8,128)(2,1)} %param.8) | copy-start | bytes 196612
  91.8 75.8 %copy-start.11 = (bf16[1,1,8,4096]{3,2,1,0:T(8,128)(2,1)S(1)}, bf16[1,1,8,4096]{3,2,1,0:T(8,128)(2,1)}, u32[]{:S(2)}) copy-start(bf16[1,1,8,4096]{3,2,1,0:T(8,128)(2,1)} %param.10) | copy-start | bytes 196612
  91.8 27.6 %collective-permute-start.3 = (bf16[32,8192]{1,0:T(8,128)(2,1)}, bf16[32,8192]{1,0:T(8,128)(2,1)S(1)}, u32[]{:S(2)}, u32[]{:S(2)}) collective-permute-start(bf16[32,8192]{1,0:T(8,128)(2,1)} %get-tuple-element.39), channel_id=1, source_target_pairs={{0,8},{8,16},{16,24},{24,0},{1,9},{9,17},{17,25},{25,1},{2,10},{10... | collective-permute-start | bytes 1572872 | tf_op jit(solution)/shard_map/ppermute | solution.py:21
  96.5 28.1 %collective-permute-start.4 = (bf16[32,8192]{1,0:T(8,128)(2,1)}, bf16[32,8192]{1,0:T(8,128)(2,1)S(1)}, u32[]{:S(2)}, u32[]{:S(2)}) collective-permute-start(bf16[32,8192]{1,0:T(8,128)(2,1)} %get-tuple-element.40), channel_id=1, source_target_pairs={{0,24},{8,0},{16,8},{24,16},{1,25},{9,1},{17,9},{25,17},{2,26},{10... | collective-permute-start | bytes 1572872 | tf_op jit(solution)/shard_map/ppermute | solution.py:21
  98.4 26.2 %collective-permute-start.5 = (bf16[32,8192]{1,0:T(8,128)(2,1)}, bf16[32,8192]{1,0:T(8,128)(2,1)S(1)}, u32[]{:S(2)}, u32[]{:S(2)}) collective-permute-start(bf16[32,8192]{1,0:T(8,128)(2,1)} %get-tuple-element.41), channel_id=1, source_target_pairs={{0,16},{8,24},{16,0},{24,8},{1,17},{9,25},{17,1},{25,9},{2,18},{10... | collective-permute-start | bytes 1572872 | tf_op jit(solution)/shard_map/ppermute | solution.py:21
  105.6 48.1 %collective-permute-start.13 = (bf16[128,1024]{1,0:T(8,128)(2,1)}, bf16[128,1024]{1,0:T(8,128)(2,1)S(1)}, u32[]{:S(2)}, u32[]{:S(2)}) collective-permute-start(bf16[128,1024]{1,0:T(8,128)(2,1)} %get-tuple-element.53), channel_id=1, source_target_pairs={{0,4},{1,5},{2,6},{3,7},{4,0},{5,1},{6,2},{7,3},{8,12},{9,13},{10,... | collective-permute-start | bytes 786440 | tf_op jit(solution)/shard_map/ppermute | solution.py:21
  108.5 49.6 %collective-permute-start.14 = (bf16[128,1024]{1,0:T(8,128)(2,1)}, bf16[128,1024]{1,0:T(8,128)(2,1)S(1)}, u32[]{:S(2)}, u32[]{:S(2)}) collective-permute-start(bf16[128,1024]{1,0:T(8,128)(2,1)} %get-tuple-element.54), channel_id=1, source_target_pairs={{0,3},{1,4},{2,5},{3,6},{4,7},{5,0},{6,1},{7,2},{8,11},{9,12},{10,... | collective-permute-start | bytes 786440 | tf_op jit(solution)/shard_map/ppermute | solution.py:21
  125.6 25.0 %copy-start.20 = (bf16[128,1024]{1,0:T(8,128)(2,1)S(1)}, bf16[128,1024]{1,0:T(8,128)(2,1)}, u32[]{:S(2)}) copy-start(bf16[128,1024]{1,0:T(8,128)(2,1)} %copy-done.19) | copy-start | bytes 786436
  125.6 28.0 %copy-start.18 = (bf16[128,1024]{1,0:T(8,128)(2,1)S(1)}, bf16[128,1024]{1,0:T(8,128)(2,1)}, u32[]{:S(2)}) copy-start(bf16[128,1024]{1,0:T(8,128)(2,1)} %copy-done.17) | copy-start | bytes 786436
  125.6 32.5 %copy-start.16 = (bf16[128,1024]{1,0:T(8,128)(2,1)S(1)}, bf16[128,1024]{1,0:T(8,128)(2,1)}, u32[]{:S(2)}) copy-start(bf16[128,1024]{1,0:T(8,128)(2,1)} %copy-done.15) | copy-start | bytes 786436
  125.6 36.0 %copy-start.14 = (bf16[128,1024]{1,0:T(8,128)(2,1)S(1)}, bf16[128,1024]{1,0:T(8,128)(2,1)}, u32[]{:S(2)}) copy-start(bf16[128,1024]{1,0:T(8,128)(2,1)} %copy-done.13) | copy-start | bytes 786436
  125.9 35.7 %collective-permute-start.9 = (bf16[2,8,4096]{2,1,0:T(8,128)(2,1)S(1)}, bf16[2,8,4096]{2,1,0:T(8,128)(2,1)S(1)}, u32[]{:S(2)}, u32[]{:S(2)}) collective-permute-start(bf16[2,8,4096]{2,1,0:T(8,128)(2,1)S(1)} %get-tuple-element.47), channel_id=1, source_target_pairs={{0,32},{32,0},{64,96},{96,64},{1,33},{33,1},{65,97},{97,65},{2,34}... | collective-permute-start | bytes 393224 | tf_op jit(solution)/shard_map/ppermute | solution.py:240
  128.3 35.7 %collective-permute-start.6 = (bf16[2,8,4096]{2,1,0:T(8,128)(2,1)S(1)}, bf16[2,8,4096]{2,1,0:T(8,128)(2,1)S(1)}, u32[]{:S(2)}, u32[]{:S(2)}) collective-permute-start(bf16[2,8,4096]{2,1,0:T(8,128)(2,1)S(1)} %get-tuple-element.43), channel_id=1, source_target_pairs={{0,96},{32,64},{64,32},{96,0},{1,97},{33,65},{65,33},{97,1},{2,98}... | collective-permute-start | bytes 393224 | tf_op jit(solution)/shard_map/ppermute | solution.py:240
  135.5 15.1 %collective-permute-start.10 = (bf16[8,4096]{1,0:T(8,128)(2,1)S(1)}, bf16[8,4096]{1,0:T(8,128)(2,1)S(1)}, u32[]{:S(2)}, u32[]{:S(2)}) collective-permute-start(bf16[8,4096]{1,0:T(8,128)(2,1)S(1)} %bitcast.31), channel_id=1, source_target_pairs={{0,96},{32,64},{64,32},{96,0},{1,97},{33,65},{65,33},{97,1},{2,98}... | collective-permute-start | bytes 196616 | tf_op jit(solution)/shard_map/ppermute | solution.py:240
  150.6 29.6 %collective-permute-start.15 = (bf16[128,1024]{1,0:T(8,128)(2,1)S(1)}, bf16[128,1024]{1,0:T(8,128)(2,1)S(1)}, u32[]{:S(2)}, u32[]{:S(2)}) collective-permute-start(bf16[128,1024]{1,0:T(8,128)(2,1)S(1)} %copy-done.20), channel_id=1, source_target_pairs={{0,5},{1,6},{2,7},{3,0},{4,1},{5,2},{6,3},{7,4},{8,13},{9,14},{10,... | collective-permute-start | bytes 786440 | tf_op jit(solution)/shard_map/ppermute | solution.py:21
  153.7 34.7 %collective-permute-start.16 = (bf16[128,1024]{1,0:T(8,128)(2,1)S(1)}, bf16[128,1024]{1,0:T(8,128)(2,1)S(1)}, u32[]{:S(2)}, u32[]{:S(2)}) collective-permute-start(bf16[128,1024]{1,0:T(8,128)(2,1)S(1)} %copy-done.18), channel_id=1, source_target_pairs={{0,2},{1,3},{2,4},{3,5},{4,6},{5,7},{6,0},{7,1},{8,10},{9,11},{10,... | collective-permute-start | bytes 786440 | tf_op jit(solution)/shard_map/ppermute | solution.py:21
  158.2 32.4 %collective-permute-start.17 = (bf16[128,1024]{1,0:T(8,128)(2,1)S(1)}, bf16[128,1024]{1,0:T(8,128)(2,1)S(1)}, u32[]{:S(2)}, u32[]{:S(2)}) collective-permute-start(bf16[128,1024]{1,0:T(8,128)(2,1)S(1)} %copy-done.16), channel_id=1, source_target_pairs={{0,6},{1,7},{2,0},{3,1},{4,2},{5,3},{6,4},{7,5},{8,14},{9,15},{10,... | collective-permute-start | bytes 786440 | tf_op jit(solution)/shard_map/ppermute | solution.py:21
  161.7 31.2 %collective-permute-start.18 = (bf16[128,1024]{1,0:T(8,128)(2,1)S(1)}, bf16[128,1024]{1,0:T(8,128)(2,1)S(1)}, u32[]{:S(2)}, u32[]{:S(2)}) collective-permute-start(bf16[128,1024]{1,0:T(8,128)(2,1)S(1)} %copy-done.14), channel_id=1, source_target_pairs={{0,1},{1,2},{2,3},{3,4},{4,5},{5,6},{6,7},{7,0},{8,9},{9,10},{10,1... | collective-permute-start | bytes 786440 | tf_op jit(solution)/shard_map/ppermute | solution.py:21
  164.0 36.2 %collective-permute-start.19 = (bf16[128,1024]{1,0:T(8,128)(2,1)S(1)}, bf16[128,1024]{1,0:T(8,128)(2,1)S(1)}, u32[]{:S(2)}, u32[]{:S(2)}) collective-permute-start(bf16[128,1024]{1,0:T(8,128)(2,1)S(1)} %get-tuple-element.59), channel_id=1, source_target_pairs={{0,7},{1,0},{2,1},{3,2},{4,3},{5,4},{6,5},{7,6},{8,15},{9,8},{10,9... | collective-permute-start | bytes 786440 | tf_op jit(solution)/shard_map/ppermute | solution.py:21
  180.2 22.1 %collective-permute-start.11 = (bf16[8,4096]{1,0:T(8,128)(2,1)S(1)}, bf16[8,4096]{1,0:T(8,128)(2,1)S(1)}, u32[]{:S(2)}, u32[]{:S(2)}) collective-permute-start(bf16[8,4096]{1,0:T(8,128)(2,1)S(1)} %get-tuple-element.48), channel_id=1, source_target_pairs={{0,896},{128,0},{256,128},{384,256},{512,384},{640,512},{768,640},... | collective-permute-start | bytes 196616 | tf_op jit(solution)/shard_map/ppermute | solution.py:21
  188.4 13.9 %collective-permute-start.12 = (bf16[8,4096]{1,0:T(8,128)(2,1)S(1)}, bf16[8,4096]{1,0:T(8,128)(2,1)S(1)}, u32[]{:S(2)}, u32[]{:S(2)}) collective-permute-start(bf16[8,4096]{1,0:T(8,128)(2,1)S(1)} %get-tuple-element.49), channel_id=1, source_target_pairs={{0,992},{32,960},{64,928},{96,896},{128,96},{160,64},{192,32},{224... | collective-permute-start | bytes 196616 | tf_op jit(solution)/shard_map/ppermute | solution.py:255
  190.6 12.4 %collective-permute-start.7 = (bf16[8,4096]{1,0:T(8,128)(2,1)S(1)}, bf16[8,4096]{1,0:T(8,128)(2,1)S(1)}, u32[]{:S(2)}, u32[]{:S(2)}) collective-permute-start(bf16[8,4096]{1,0:T(8,128)(2,1)S(1)} %get-tuple-element.44), channel_id=1, source_target_pairs={{0,128},{128,256},{256,384},{384,512},{512,640},{640,768},{768,896... | collective-permute-start | bytes 196616 | tf_op jit(solution)/shard_map/ppermute | solution.py:21
  192.8 15.2 %collective-permute-start.8 = (bf16[8,4096]{1,0:T(8,128)(2,1)S(1)}, bf16[8,4096]{1,0:T(8,128)(2,1)S(1)}, u32[]{:S(2)}, u32[]{:S(2)}) collective-permute-start(bf16[8,4096]{1,0:T(8,128)(2,1)S(1)} %get-tuple-element.45), channel_id=1, source_target_pairs={{0,160},{32,128},{64,224},{96,192},{128,288},{160,256},{192,352},{... | collective-permute-start | bytes 196616 | tf_op jit(solution)/shard_map/ppermute | solution.py:255
  (9 other events, 7.3 us)
